TPU v7x, 32 devices: a whole 2x2x4 slice. The times are simulated.
32 devices in a mesh: dp: 8 (over y, x, core), mp: 4 (over z).
Axes of the slice: x: 2, y: 2, z: 4, core: 2. Of those that a mesh axis runs over, the one named last changes fastest.
Arguments:
- tokens: bfloat16 [2048, 6144], P('dp', 'mp'), may hold values from -40 to 40
- norm_gain: float32 [6144], P('mp'), may hold values from 0.1 to 1.9
- w_qkv: bfloat16 [6144, 3, 4096], P('mp', None, 'dp'), may hold values from -0.078125 to 0.078125
- w_up: bfloat16 [6144, 12288], P('mp', 'dp'), may hold values from -0.078125 to 0.078125
- w_attn_out: bfloat16 [4096, 6144], P('dp', 'mp'), may hold values from -0.09375 to 0.09375
- w_down: bfloat16 [12288, 6144], P('dp', 'mp'), may hold values from -0.0546875 to 0.0546875
Outputs:
- layer_out: bfloat16 [2048, 6144], P('dp', 'mp')
All inputs are finite; a program needn't handle non-finite values.
Results may differ from a plain program's by a relative error of at most 0.015.
Values may be sent and summed in bfloat16 or wider, within the bound.
A program may use at most 128 MiB of HBM per device.

v0:
```python
import jax
import jax.numpy as jnp
from jax import lax
from jax.sharding import PartitionSpec as P

HEAD_DIM = 128
PATCHES = 256
EPS = 1e-06


def normalize_rows(values, total, squares, gain, width):
    mean = total / width
    spread = squares / width - mean * mean
    scaled = (values - mean[:, None]) * lax.rsqrt(spread + EPS)[:, None]
    return (scaled * gain[None, :]).astype(jnp.bfloat16)


def head_norm(values):
    mean = jnp.mean(values, axis=-1, keepdims=True)
    centered = values - mean
    spread = jnp.mean(centered * centered, axis=-1, keepdims=True)
    return centered * lax.rsqrt(spread + EPS)


def attend(qkv, heads_here):
    rows = qkv.shape[0]
    images = rows // PATCHES
    parts = qkv.reshape(images, PATCHES, 3, heads_here, HEAD_DIM)
    query = (head_norm(parts[:, :, 0].astype(jnp.float32)) * (1.0 / HEAD_DIM) ** 0.5).astype(
        jnp.bfloat16
    )
    keys = head_norm(parts[:, :, 1].astype(jnp.float32)).astype(jnp.bfloat16)
    values = parts[:, :, 2]
    scores = jnp.einsum("iqhd,ikhd->ihqk", query, keys, preferred_element_type=jnp.float32)
    weights = jnp.exp(scores)
    probs = (weights / jnp.sum(weights, axis=-1, keepdims=True)).astype(jnp.bfloat16)
    mixed = jnp.einsum("ihqk,ikhd->iqhd", probs, values, preferred_element_type=jnp.float32)
    return mixed.astype(jnp.bfloat16).reshape(rows, heads_here * HEAD_DIM)


def local(tokens, norm_gain, w_qkv, w_up, w_attn_out, w_down):
    n_mp = lax.axis_size("mp")
    feat_here = tokens.shape[1]
    head_cols = w_qkv.shape[2]
    heads_here = head_cols // HEAD_DIM
    width = feat_here * n_mp
    tokens_f = tokens.astype(jnp.float32)
    total, squares = lax.psum(
        (jnp.sum(tokens_f, axis=1), jnp.sum(tokens_f * tokens_f, axis=1)), "mp"
    )
    normed = normalize_rows(tokens_f, total, squares, norm_gain, width)
    normed_all = lax.all_gather(normed, "dp", axis=0, tiled=True)
    w_heads = w_qkv.reshape(feat_here, 3 * head_cols)
    projected = lax.psum_scatter(
        jnp.concatenate(
            [
                jnp.dot(normed_all, w_heads, preferred_element_type=jnp.float32),
                jnp.dot(normed_all, w_up, preferred_element_type=jnp.float32),
            ],
            axis=1,
        ).astype(jnp.bfloat16),
        "mp",
        scatter_dimension=0,
        tiled=True,
    )
    qkv = projected[:, : 3 * head_cols].reshape(projected.shape[0], 3, head_cols)
    attended = attend(qkv, heads_here)
    activated = jax.nn.gelu(projected[:, 3 * head_cols :].astype(jnp.float32)).astype(jnp.bfloat16)
    hidden = jnp.concatenate([attended, activated], axis=1)
    piece = lax.all_gather(hidden, "mp", axis=0, tiled=True)
    result = jnp.dot(piece[:, :head_cols], w_attn_out, preferred_element_type=jnp.float32)
    partial_out = result + jnp.dot(piece[:, head_cols:], w_down, preferred_element_type=jnp.float32)
    summed = lax.psum_scatter(
        partial_out.astype(jnp.bfloat16), "dp", scatter_dimension=0, tiled=True
    ).astype(jnp.float32)
    return (tokens_f + summed).astype(jnp.bfloat16)


def solution(mesh):
    placed = (
        P("dp", "mp"),
        P("mp"),
        P("mp", None, "dp"),
        P("mp", "dp"),
        P("dp", "mp"),
        P("dp", "mp"),
    )
    return jax.shard_map(
        local, mesh=mesh, in_specs=placed, out_specs=P("dp", "mp"), check_vma=False
    )
```

profile of v0, /device:TPU:0, one launch (start us, length us, event | category | flops | bytes accessed | tf_op | source)
XLA Modules:
  0.0 583.7 jit_solution(13878567147038606246)
XLA Ops:
  6.5 0.0 copy-start
  6.5 0.0 all-gather.3.cloned.1.call-start
  6.5 1.6 convert_reduce_fusion
  8.1 13.5 %all-reduce = (f32[256]{0:T(256)S(1)}, f32[256]{0:T(256)S(1)}) all-reduce(f32[256]{0:T(256)S(1)} %get-tuple-element.6, f32[256]{0:T(256)S(1)} %get-tuple-element.5), channel_id=1, replica_groups=mesh['dp'=8,'mp'=4] {'mp'}, use_global_device_ids=true, to_apply=%region_3.0 | all-reduce | flops 512 | bytes 4096 | tf_op jit(solution)/shard_map/psum | solution.py:48
  21.6 2.3 fusion.11
  24.0 0.0 all-gather.3.cloned.1.call-update
  24.0 0.0 reduce-scatter.3.cloned.1.call-start
  24.0 6.8 %copy.12 = bf16[1536,3,512]{0,2,1:T(8,128)(2,1)} copy(bf16[1536,3,512]{2,0,1:T(8,128)(2,1)} %param.8) | data formatting | bytes 9437184 | tf_op args[2]
  30.8 36.9 %all-gather.3.cloned.1.call-done = bf16[2048,1536]{1,0:T(8,128)(2,1)} async-done(((bf16[256,1536]{1,0:T(8,128)(2,1)}), bf16[2048,1536]{1,0:T(8,128)(2,1)}) %all-gather.3.cloned.1.call-update) | async-done | bytes 6291472 | tf_op jit(solution)/shard_map/all_gather | solution.py:52
  67.7 13.5 %convolution_convert_fusion.1 = bf16[2048,1536]{0,1:T(8,128)(2,1)S(1)} fusion(bf16[2048,1536]{1,0:T(8,128)(2,1)} %all-gather.3.cloned.1.call-done, bf16[1536,1536]{0,1:T(8,128)(2,1)} %bitcast.51), kind=kOutput, calls=%fused_computation.3 | convolution fusion | flops 9666822144 | bytes 17301504 | tf_op jit(solution)/shard_map/dot_general | solution.py:57
  81.3 13.5 %convolution_convert_fusion = bf16[2048,1536]{0,1:T(8,128)(2,1)S(1)} fusion(bf16[2048,1536]{1,0:T(8,128)(2,1)} %all-gather.3.cloned.1.call-done, bf16[1536,1536]{1,0:T(8,128)(2,1)} %param.9), kind=kOutput, calls=%fused_computation.2 | convolution fusion | flops 9666822144 | bytes 17301504 | tf_op jit(solution)/shard_map/dot_general | solution.py:58
  94.8 14.5 %pad_maximum_fusion = bf16[2048,3072]{0,1:T(8,128)(2,1)} fusion(bf16[2048,1536]{0,1:T(8,128)(2,1)S(1)} %convolution_convert_fusion, bf16[2048,1536]{0,1:T(8,128)(2,1)S(1)} %convolution_convert_fusion.1), kind=kLoop, calls=%fused_computation | loop fusion | flops 25165824 | bytes 25165824 | tf_op jit(solution)/shard_map/concatenate | solution.py:55
  109.4 0.0 reduce-scatter.3.cloned.1.call-update
  109.4 0.2 all-gather.5.cloned.1.call-start
  109.6 211.8 %reduce-scatter.3.cloned.1.call-done = bf16[512,3072]{0,1:T(8,128)(2,1)} async-done(((bf16[2048,3072]{0,1:T(8,128)(2,1)}), bf16[512,3072]{0,1:T(8,128)(2,1)}) %reduce-scatter.3.cloned.1.call-update) | async-done | bytes 3145744 | tf_op jit(solution)/shard_map/reduce_scatter | solution.py:54
  321.4 2.7 slice.28
  324.1 2.4 reshape_reshape.3
  326.4 2.2 fusion.35
  328.6 1.4 copy.21
  330.0 0.2 convert_reduce_fusion.1
  330.2 0.0 copy-start.3
  330.2 0.7 fusion.24
  330.9 1.4 copy.20
  332.2 0.2 convert_reduce_fusion.2
  332.4 0.7 fusion.18
  333.1 2.8 exponential_reduce_fusion
  335.9 0.0 copy-done.3
  336.0 0.0 copy-start.2
  336.0 0.5 fusion.14
  336.5 0.5 copy.17
  337.0 0.1 copy.22
  337.1 0.7 copy-done.2
  337.8 1.1 fusion.6
  338.9 1.5 pad_maximum_fusion.1
  340.4 0.0 all-gather.5.cloned.1.call-update
  340.4 0.0 reduce-scatter.5.cloned.1.call-start
  340.5 150.8 %all-gather.5.cloned.1.call-done = bf16[2048,2048]{0,1:T(8,128)(2,1)} async-done(((bf16[512,2048]{0,1:T(8,128)(2,1)}), bf16[2048,2048]{0,1:T(8,128)(2,1)}) %all-gather.5.cloned.1.call-update) | async-done | bytes 8388624 | tf_op jit(solution)/shard_map/all_gather | solution.py:70
  491.3 0.0 copy-done
  491.3 0.0 copy-start.4
  491.3 8.2 %fusion.7 = f32[2048,1536]{1,0:T(8,128)} fusion(bf16[512,1536]{1,0:T(8,128)(2,1)S(1)} %copy-done, bf16[2048,2048]{0,1:T(8,128)(2,1)} %all-gather.5.cloned.1.call-done), kind=kOutput, calls=%fused_computation.19 | convolution fusion | flops 3221225472 | bytes 16252928 | tf_op jit(solution)/shard_map/dot_general | solution.py:71
  499.5 0.0 copy-done.4
  499.5 15.3 %add_convert_fusion = bf16[2048,1536]{1,0:T(8,128)(2,1)} fusion(f32[2048,1536]{1,0:T(8,128)} %fusion.7, bf16[1536,1536]{1,0:T(8,128)(2,1)} %param.11, bf16[2048,2048]{0,1:T(8,128)(2,1)S(1)} %copy-done.4), kind=kOutput, calls=%fused_computation.1 | convolution fusion | flops 9669967872 | bytes 29884416 | tf_op jit(solution)/shard_map/dot_general | solution.py:72
  514.8 0.0 copy-start.1
  514.8 0.0 reduce-scatter.5.cloned.1.call-update
  514.9 60.1 %reduce-scatter.5.cloned.1.call-done = bf16[256,1536]{1,0:T(8,128)(2,1)} async-done(((bf16[2048,1536]{1,0:T(8,128)(2,1)}), bf16[256,1536]{1,0:T(8,128)(2,1)}) %reduce-scatter.5.cloned.1.call-update) | async-done | bytes 786448 | tf_op jit(solution)/shard_map/reduce_scatter | solution.py:73
  575.0 0.0 copy-done.1
  575.0 2.2 fusion.13
  (4 shorter events, 0.0 us)
Async XLA Ops:
  6.5 484.7 %copy-start = (bf16[512,1536]{1,0:T(8,128)(2,1)S(1)}, bf16[512,1536]{1,0:T(8,128)(2,1)}, u32[]{:S(2)}) copy-start(bf16[512,1536]{1,0:T(8,128)(2,1)} %param.10) | copy-start | bytes 4718596
  6.5 61.2 %all-gather.3.cloned.1.call-start = ((), (), s32[]{:S(2)}) async-start(), calls=%async_computation.2 | async-start | bytes 7077888 | tf_op jit(solution)/shard_map/all_gather | solution.py:52
  24.0 297.4 %reduce-scatter.3.cloned.1.call-start = ((), (), s32[]{:S(2)}) async-start(), calls=%async_computation.3 | async-start | bytes 15728640 | tf_op jit(solution)/shard_map/reduce_scatter | solution.py:54
  109.4 381.9 %all-gather.5.cloned.1.call-start = ((), (), s32[]{:S(2)}) async-start(), calls=%async_computation.4 | async-start | bytes 10485760 | tf_op jit(solution)/shard_map/all_gather | solution.py:70
  330.2 5.8 copy-start.3
  336.0 1.9 copy-start.2
  340.4 234.5 %reduce-scatter.5.cloned.1.call-start = ((), (), s32[]{:S(2)}) async-start(), calls=%async_computation.5 | async-start | bytes 7077888 | tf_op jit(solution)/shard_map/reduce_scatter | solution.py:73
  491.3 8.2 %copy-start.4 = (bf16[2048,2048]{0,1:T(8,128)(2,1)S(1)}, bf16[2048,2048]{0,1:T(8,128)(2,1)}, u32[]{:S(2)}) copy-start(bf16[2048,2048]{0,1:T(8,128)(2,1)} %all-gather.5.cloned.1.call-done) | copy-start | bytes 25165828
  514.8 60.1 %copy-start.1 = (bf16[256,1536]{1,0:T(8,128)(2,1)S(1)}, bf16[256,1536]{1,0:T(8,128)(2,1)}, u32[]{:S(2)}) copy-start(bf16[256,1536]{1,0:T(8,128)(2,1)} %param.6) | copy-start | bytes 2359300
Sparse Core Ops, SparseCore 0:
  24.1 43.5 all-gather.2
  109.5 211.8 reduce-scatter.2
  340.6 150.6 all-gather.4
  515.0 59.9 reduce-scatter.4
where the time goes:
time: 584 us
  waiting for transfers between devices  460 us (79%)
  matrix products  53.9 us (9%)
  other arithmetic  25 us (4%)
  local copies, waits for them, and re-layouts  18 us (3%)
  blocking collectives  13.5 us (2%)
  between operations  13.3 us (2%)
    reduce_scatter x1, waiting for transfers between devices, local(): lax.psum_scatter(jnp.concatenate([jnp.dot(normed_all, w_heads, preferred_...  212 us
    all_gather x1, waiting for transfers between devices, local(): piece = lax.all_gather(hidden, 'mp', axis=0, tiled=True)  151 us
    reduce_scatter x1, waiting for transfers between devices, local(): lax.psum_scatter(partial_out.astype(jnp.bfloat16), 'dp', scatter_dimensio...  60.1 us
    all_gather x1, waiting for transfers between devices, local(): normed_all = lax.all_gather(normed, 'dp', axis=0, tiled=True)  36.9 us
    dot_general x1, matrix products, local(): jnp.dot(piece[:, head_cols:], w_down, preferred_element_type=jnp.float32)  15.3 us
    concatenate x1, other arithmetic, local(): jnp.concatenate([jnp.dot(normed_all, w_heads, preferred_element_type=jnp....  14.5 us
    dot_general x1, matrix products, local(): jnp.dot(normed_all, w_heads, preferred_element_type=jnp.float32)  13.5 us
    dot_general x1, matrix products, local(): jnp.dot(normed_all, w_up, preferred_element_type=jnp.float32)  13.5 us
  transfers between devices with their start and end apart: 4, of which 4 were waited for; matrix products, arithmetic and copies ran while one was open for 1% of the time, Pallas kernels for 0%

commit v1 on v0

--- a/solution.py
+++ b/solution.py
@@ -49,7 +49,14 @@
         (jnp.sum(tokens_f, axis=1), jnp.sum(tokens_f * tokens_f, axis=1)), "mp"
     )
     normed = normalize_rows(tokens_f, total, squares, norm_gain, width)
-    normed_all = lax.all_gather(normed, "dp", axis=0, tiled=True)
+    size = lax.axis_size("dp")
+    right = [(i, (i + 1) % size) for i in range(size)]
+    pieces = [normed]
+    for stride in range(1, size):
+        pieces = [lax.ppermute(pieces[0], "dp", right), *pieces]
+    whole = jnp.concatenate(pieces, axis=0)
+    shift = (lax.axis_index("dp") + 1) * pieces[-1].shape[0]
+    normed_all = jnp.roll(whole, shift, axis=0)
     w_heads = w_qkv.reshape(feat_here, 3 * head_cols)
     projected = lax.psum_scatter(
         jnp.concatenate(

time: 584 us -> 640 us (1.096)
  waiting for transfers between devices: 460 us -> 500 us
  local copies, waits for them, and re-layouts: 18 us -> 34 us
    ppermute x0 -> x7, waiting for transfers between devices: none -> 79.9 us  [local(): pieces = [lax.ppermute(pieces[0], 'dp', right), *pieces]]
    all_gather x1 -> x0, waiting for transfers between devices: 36.9 us -> none  [local(): normed_all = lax.all_gather(normed, 'dp', axis=0, tiled=True)]
    unnamed x14 -> x50, local copies, waits for them, and re-layouts: 10.3 us -> 23.6 us
  transfers between devices with their start and end apart: 4 -> 10, of which waited for: 4 -> 10; matrix products, arithmetic and copies ran while one was open for 1% -> 1% of each run, Pallas kernels for 0% -> 0%
where the time goes in v1:
time: 640 us
  waiting for transfers between devices  500 us (78%)
  matrix products  53.6 us (8%)
  local copies, waits for them, and re-layouts  34 us (5%)
  other arithmetic  24.9 us (4%)
  blocking collectives  13.5 us (2%)
  between operations  13.4 us (2%)
    reduce_scatter x1, waiting for transfers between devices, local(): lax.psum_scatter(jnp.concatenate([jnp.dot(normed_all, w_heads, preferred_...  209 us
    all_gather x1, waiting for transfers between devices, local(): piece = lax.all_gather(hidden, 'mp', axis=0, tiled=True)  151 us
    ppermute x7, waiting for transfers between devices, local(): pieces = [lax.ppermute(pieces[0], 'dp', right), *pieces]  79.9 us
    reduce_scatter x1, waiting for transfers between devices, local(): lax.psum_scatter(partial_out.astype(jnp.bfloat16), 'dp', scatter_dimensio...  60.1 us
    unnamed x50, local copies, waits for them, and re-layouts  23.6 us
    dot_general x1, matrix products, local(): jnp.dot(piece[:, head_cols:], w_down, preferred_element_type=jnp.float32)  15.3 us
    concatenate x1, other arithmetic, local(): jnp.concatenate([jnp.dot(normed_all, w_heads, preferred_element_type=jnp....  14.8 us
    dot_general x1, matrix products, local(): jnp.dot(normed_all, w_up, preferred_element_type=jnp.float32)  13.5 us
  transfers between devices with their start and end apart: 10, of which 10 were waited for; matrix products, arithmetic and copies ran while one was open for 1% of the time, Pallas kernels for 0%

profile of v1, /device:TPU:0, one launch (start us, length us, event | category | flops | bytes accessed | tf_op | source)
XLA Modules:
  0.0 639.8 jit_solution(10740868780414307128)
XLA Ops:
  6.5 1.6 convert_reduce_fusion
  8.1 13.5 %all-reduce = (f32[256]{0:T(256)S(1)}, f32[256]{0:T(256)S(1)}) all-reduce(f32[256]{0:T(256)S(1)} %get-tuple-element.6, f32[256]{0:T(256)S(1)} %get-tuple-element.5), channel_id=1, replica_groups=mesh['dp'=8,'mp'=4] {'mp'}, use_global_device_ids=true, to_apply=%region_3.0 | all-reduce | flops 512 | bytes 4096 | tf_op jit(solution)/shard_map/psum | solution.py:48
  21.6 1.4 fusion.13
  23.1 0.1 collective-permute-start
  23.2 12.3 %collective-permute-done = bf16[256,1536]{1,0:T(8,128)(2,1)S(1)} collective-permute-done((bf16[256,1536]{1,0:T(8,128)(2,1)S(1)}, bf16[256,1536]{1,0:T(8,128)(2,1)S(1)}, u32[]{:S(2)}, u32[]{:S(2)}) %collective-permute-start) | collective-permute-done | bytes 786464 | tf_op jit(solution)/shard_map/ppermute | solution.py:56
  35.5 12.3 %collective-permute-done.1 = bf16[256,1536]{1,0:T(8,128)(2,1)S(1)} collective-permute-done((bf16[256,1536]{1,0:T(8,128)(2,1)S(1)}, bf16[256,1536]{1,0:T(8,128)(2,1)S(1)}, u32[]{:S(2)}, u32[]{:S(2)}) %collective-permute-start.1) | collective-permute-done | bytes 786464 | tf_op jit(solution)/shard_map/ppermute | solution.py:56
  47.8 12.3 %collective-permute-done.2 = bf16[256,1536]{1,0:T(8,128)(2,1)S(1)} collective-permute-done((bf16[256,1536]{1,0:T(8,128)(2,1)S(1)}, bf16[256,1536]{1,0:T(8,128)(2,1)S(1)}, u32[]{:S(2)}, u32[]{:S(2)}) %collective-permute-start.2) | collective-permute-done | bytes 786464 | tf_op jit(solution)/shard_map/ppermute | solution.py:56
  60.1 0.9 copy-done.5
  61.0 0.0 collective-permute-start.3
  61.0 12.3 %collective-permute-done.3 = bf16[256,1536]{1,0:T(8,128)(2,1)S(1)} collective-permute-done((bf16[256,1536]{1,0:T(8,128)(2,1)S(1)}, bf16[256,1536]{1,0:T(8,128)(2,1)S(1)}, u32[]{:S(2)}, u32[]{:S(2)}) %collective-permute-start.3) | collective-permute-done | bytes 786464 | tf_op jit(solution)/shard_map/ppermute | solution.py:56
  73.3 0.9 copy-done.7
  74.2 0.0 collective-permute-start.4
  74.2 12.3 %collective-permute-done.4 = bf16[256,1536]{1,0:T(8,128)(2,1)S(1)} collective-permute-done((bf16[256,1536]{1,0:T(8,128)(2,1)S(1)}, bf16[256,1536]{1,0:T(8,128)(2,1)S(1)}, u32[]{:S(2)}, u32[]{:S(2)}) %collective-permute-start.4) | collective-permute-done | bytes 786464 | tf_op jit(solution)/shard_map/ppermute | solution.py:56
  86.5 0.9 copy-done.9
  87.4 12.4 %collective-permute-done.5 = bf16[256,1536]{1,0:T(8,128)(2,1)} collective-permute-done((bf16[256,1536]{1,0:T(8,128)(2,1)S(1)}, bf16[256,1536]{1,0:T(8,128)(2,1)}, u32[]{:S(2)}, u32[]{:S(2)}) %collective-permute-start.5) | collective-permute-done | bytes 786464 | tf_op jit(solution)/shard_map/ppermute | solution.py:56
  99.8 6.6 %copy.12 = bf16[1536,3,512]{0,2,1:T(8,128)(2,1)} copy(bf16[1536,3,512]{2,0,1:T(8,128)(2,1)} %param.8) | data formatting | bytes 9437184 | tf_op args[2]
  106.4 6.0 collective-permute-done.6
  112.4 1.2 constant_dynamic-update-slice_fusion.15
  113.6 1.2 constant_dynamic-update-slice_fusion.14
  114.8 0.0 copy-start.10
  114.8 1.3 constant_dynamic-update-slice_fusion.13
  116.1 1.3 constant_dynamic-update-slice_fusion.12
  117.3 0.1 constant_dynamic-update-slice_fusion.11
  117.4 0.1 constant_dynamic-update-slice_fusion.10
  117.5 0.1 constant_dynamic-update-slice_fusion.9
  117.6 0.3 constant_dynamic-update-slice_fusion.8
  117.9 1.3 constant_dynamic-update-slice_fusion.7
  119.2 1.2 constant_dynamic-update-slice_fusion.6
  120.4 0.1 constant_dynamic-update-slice_fusion.5
  120.5 0.1 constant_dynamic-update-slice_fusion.4
  120.6 0.1 constant_dynamic-update-slice_fusion.3
  120.6 0.1 constant_dynamic-update-slice_fusion.2
  120.7 0.1 constant_dynamic-update-slice_fusion.1
  120.8 0.3 constant_dynamic-update-slice_fusion
  121.1 4.5 copy-done.12
  125.6 12.1 %convolution_convert_fusion.1 = bf16[2048,1536]{0,1:T(8,128)(2,1)S(1)} fusion(bf16[1536,1536]{0,1:T(8,128)(2,1)S(1)} %bitcast.51, bf16[4096,1536]{1,0:T(8,128)(2,1)} %copy-done.12, s32[]{:T(128)S(6)} %select_n.14), kind=kOutput, calls=%fused_computation.3 | convolution fusion | flops 9666822144 | bytes 17301508 | tf_op jit(solution)/shard_map/dot_general | solution.py:64
  137.7 13.5 %convolution_convert_fusion = bf16[2048,1536]{0,1:T(8,128)(2,1)S(1)} fusion(bf16[1536,1536]{1,0:T(8,128)(2,1)} %param.9, bf16[4096,1536]{1,0:T(8,128)(2,1)} %copy-done.12, s32[]{:T(128)S(6)} %select_n.14), kind=kOutput, calls=%fused_computation.2 | convolution fusion | flops 9666822144 | bytes 17301508 | tf_op jit(solution)/shard_map/dot_general | solution.py:65
  151.3 14.8 %pad_maximum_fusion = bf16[2048,3072]{0,1:T(8,128)(2,1)} fusion(bf16[2048,1536]{0,1:T(8,128)(2,1)S(1)} %convolution_convert_fusion, bf16[2048,1536]{0,1:T(8,128)(2,1)S(1)} %convolution_convert_fusion.1), kind=kLoop, calls=%fused_computation | loop fusion | flops 25165824 | bytes 25165824 | tf_op jit(solution)/shard_map/concatenate | solution.py:62
  166.0 0.0 reduce-scatter.3.cloned.1.call-update
  166.1 0.0 all-gather.2.cloned.1.call-start
  166.1 209.3 %reduce-scatter.3.cloned.1.call-done = bf16[512,3072]{0,1:T(8,128)(2,1)} async-done(((bf16[2048,3072]{0,1:T(8,128)(2,1)}), bf16[512,3072]{0,1:T(8,128)(2,1)}) %reduce-scatter.3.cloned.1.call-update) | async-done | bytes 3145744 | tf_op jit(solution)/shard_map/reduce_scatter | solution.py:61
  375.4 2.7 slice.28
  378.0 3.5 reshape_reshape.3
  381.6 3.6 fusion.39
  385.2 0.5 copy.20
  385.7 0.2 convert_reduce_fusion.2
  385.9 0.7 fusion.20
  386.6 1.4 copy.21
  387.9 0.2 convert_reduce_fusion.1
  388.2 0.7 fusion.26
  388.9 2.8 exponential_reduce_fusion
  391.7 1.6 fusion.16
  393.2 0.5 copy.17
  393.8 0.1 copy.22
  393.9 1.1 fusion.8
  395.0 1.5 pad_maximum_fusion.1
  396.4 0.0 all-gather.2.cloned.1.call-update
  396.5 0.0 reduce-scatter.5.cloned.1.call-start
  396.5 150.8 %all-gather.2.cloned.1.call-done = bf16[2048,2048]{0,1:T(8,128)(2,1)} async-done(((bf16[512,2048]{0,1:T(8,128)(2,1)}), bf16[2048,2048]{0,1:T(8,128)(2,1)}) %all-gather.2.cloned.1.call-update) | async-done | bytes 8388624 | tf_op jit(solution)/shard_map/all_gather | solution.py:77
  547.3 8.3 %fusion.9 = f32[2048,1536]{1,0:T(8,128)} fusion(bf16[512,1536]{1,0:T(8,128)(2,1)S(1)} %copy-done, bf16[2048,2048]{0,1:T(8,128)(2,1)} %all-gather.2.cloned.1.call-done), kind=kOutput, calls=%fused_computation.21 | convolution fusion | flops 3221225472 | bytes 16252928 | tf_op jit(solution)/shard_map/dot_general | solution.py:78
  555.6 15.3 %add_convert_fusion = bf16[2048,1536]{1,0:T(8,128)(2,1)} fusion(f32[2048,1536]{1,0:T(8,128)} %fusion.9, bf16[1536,1536]{1,0:T(8,128)(2,1)} %param.11, bf16[2048,2048]{0,1:T(8,128)(2,1)S(1)} %copy-done.13), kind=kOutput, calls=%fused_computation.1 | convolution fusion | flops 9669967872 | bytes 29884416 | tf_op jit(solution)/shard_map/dot_general | solution.py:79
  570.9 0.0 reduce-scatter.5.cloned.1.call-update
  570.9 60.1 %reduce-scatter.5.cloned.1.call-done = bf16[256,1536]{1,0:T(8,128)(2,1)} async-done(((bf16[2048,1536]{1,0:T(8,128)(2,1)}), bf16[256,1536]{1,0:T(8,128)(2,1)}) %reduce-scatter.5.cloned.1.call-update) | async-done | bytes 786448 | tf_op jit(solution)/shard_map/reduce_scatter | solution.py:80
  631.0 2.2 fusion.15
  (37 shorter events, 0.1 us)
Async XLA Ops:
  6.5 540.7 %copy-start = (bf16[512,1536]{1,0:T(8,128)(2,1)S(1)}, bf16[512,1536]{1,0:T(8,128)(2,1)}, u32[]{:S(2)}) copy-start(bf16[512,1536]{1,0:T(8,128)(2,1)} %param.10) | copy-start | bytes 4718596
  6.5 368.8 %reduce-scatter.3.cloned.1.call-start = ((), (), s32[]{:S(2)}) async-start(), calls=%async_computation.2 | async-start | bytes 15728640 | tf_op jit(solution)/shard_map/reduce_scatter | solution.py:61
  23.1 12.4 %collective-permute-start = (bf16[256,1536]{1,0:T(8,128)(2,1)S(1)}, bf16[256,1536]{1,0:T(8,128)(2,1)S(1)}, u32[]{:S(2)}, u32[]{:S(2)}) collective-permute-start(bf16[256,1536]{1,0:T(8,128)(2,1)S(1)} %fusion.13), channel_id=1, source_target_pairs={{0,4},{4,8},{8,12},{12,16},{16,20},{20,24},{24,28},{28,0},{1,5},{5... | collective-permute-start | bytes 2359304 | tf_op jit(solution)/shard_map/ppermute | solution.py:56
  35.5 12.3 %collective-permute-start.1 = (bf16[256,1536]{1,0:T(8,128)(2,1)S(1)}, bf16[256,1536]{1,0:T(8,128)(2,1)S(1)}, u32[]{:S(2)}, u32[]{:S(2)}) collective-permute-start(bf16[256,1536]{1,0:T(8,128)(2,1)S(1)} %collective-permute-done), channel_id=1, source_target_pairs={{0,4},{4,8},{8,12},{12,16},{16,20},{20,24},{24,28},{28,0},{1,5},{5... | collective-permute-start | bytes 2359304 | tf_op jit(solution)/shard_map/ppermute | solution.py:56
  47.8 52.0 %copy-start.3 = (bf16[256,1536]{1,0:T(8,128)(2,1)}, bf16[256,1536]{1,0:T(8,128)(2,1)S(1)}, u32[]{:S(2)}) copy-start(bf16[256,1536]{1,0:T(8,128)(2,1)S(1)} %collective-permute-done.1) | copy-start | bytes 2359300
  47.8 12.3 %collective-permute-start.2 = (bf16[256,1536]{1,0:T(8,128)(2,1)S(1)}, bf16[256,1536]{1,0:T(8,128)(2,1)S(1)}, u32[]{:S(2)}, u32[]{:S(2)}) collective-permute-start(bf16[256,1536]{1,0:T(8,128)(2,1)S(1)} %collective-permute-done.1), channel_id=1, source_target_pairs={{0,4},{4,8},{8,12},{12,16},{16,20},{20,24},{24,28},{28,0},{1,5},{5... | collective-permute-start | bytes 2359304 | tf_op jit(solution)/shard_map/ppermute | solution.py:56
  60.1 0.9 copy-start.5
  61.0 12.3 %collective-permute-start.3 = (bf16[256,1536]{1,0:T(8,128)(2,1)S(1)}, bf16[256,1536]{1,0:T(8,128)(2,1)S(1)}, u32[]{:S(2)}, u32[]{:S(2)}) collective-permute-start(bf16[256,1536]{1,0:T(8,128)(2,1)S(1)} %collective-permute-done.2), channel_id=1, source_target_pairs={{0,4},{4,8},{8,12},{12,16},{16,20},{20,24},{24,28},{28,0},{1,5},{5... | collective-permute-start | bytes 2359304 | tf_op jit(solution)/shard_map/ppermute | solution.py:56
  73.3 0.9 copy-start.7
  74.2 12.3 %collective-permute-start.4 = (bf16[256,1536]{1,0:T(8,128)(2,1)S(1)}, bf16[256,1536]{1,0:T(8,128)(2,1)S(1)}, u32[]{:S(2)}, u32[]{:S(2)}) collective-permute-start(bf16[256,1536]{1,0:T(8,128)(2,1)S(1)} %collective-permute-done.3), channel_id=1, source_target_pairs={{0,4},{4,8},{8,12},{12,16},{16,20},{20,24},{24,28},{28,0},{1,5},{5... | collective-permute-start | bytes 2359304 | tf_op jit(solution)/shard_map/ppermute | solution.py:56
  86.5 0.9 copy-start.9
  87.4 12.4 %collective-permute-start.5 = (bf16[256,1536]{1,0:T(8,128)(2,1)S(1)}, bf16[256,1536]{1,0:T(8,128)(2,1)}, u32[]{:S(2)}, u32[]{:S(2)}) collective-permute-start(bf16[256,1536]{1,0:T(8,128)(2,1)S(1)} %collective-permute-done.4), channel_id=1, source_target_pairs={{0,4},{4,8},{8,12},{12,16},{16,20},{20,24},{24,28},{28,0},{1,5},{5... | collective-permute-start | bytes 2359304 | tf_op jit(solution)/shard_map/ppermute | solution.py:56
  99.8 12.6 %collective-permute-start.6 = (bf16[256,1536]{1,0:T(8,128)(2,1)}, bf16[256,1536]{1,0:T(8,128)(2,1)}, u32[]{:S(2)}, u32[]{:S(2)}) collective-permute-start(bf16[256,1536]{1,0:T(8,128)(2,1)} %collective-permute-done.5), channel_id=1, source_target_pairs={{0,4},{4,8},{8,12},{12,16},{16,20},{20,24},{24,28},{28,0},{1,5},{5... | collective-permute-start | bytes 2359304 | tf_op jit(solution)/shard_map/ppermute | solution.py:56
  106.4 11.1 %copy-start.1 = (bf16[256,1536]{1,0:T(8,128)(2,1)S(1)}, bf16[256,1536]{1,0:T(8,128)(2,1)}, u32[]{:S(2)}) copy-start(bf16[256,1536]{1,0:T(8,128)(2,1)} %param.6) | copy-start | bytes 2359300
  106.4 11.1 %copy-start.11 = (f32[1536]{0:T(1024)S(1)}, f32[1536]{0:T(1024)}, u32[]{:S(2)}) copy-start(f32[1536]{0:T(1024)} %param.7) | copy-start | bytes 18436
  106.4 10.9 %copy-start.6 = (bf16[256,1536]{1,0:T(8,128)(2,1)S(1)}, bf16[256,1536]{1,0:T(8,128)(2,1)}, u32[]{:S(2)}) copy-start(bf16[256,1536]{1,0:T(8,128)(2,1)} %copy-done.5) | copy-start | bytes 2359300
  106.4 11.0 %copy-start.4 = (bf16[256,1536]{1,0:T(8,128)(2,1)S(1)}, bf16[256,1536]{1,0:T(8,128)(2,1)}, u32[]{:S(2)}) copy-start(bf16[256,1536]{1,0:T(8,128)(2,1)} %copy-done.3) | copy-start | bytes 2359300
  114.8 5.6 copy-start.10
  116.1 4.4 copy-start.8
  117.6 8.0 %slice-start = ((s8[4718592]{0:T(1024)(128)(4,1)}), s8[4194304]{0:T(1024)(128)(4,1)S(1)}, s32[]{:S(2)}) async-start(s8[4718592]{0:T(1024)(128)(4,1)} %bitcast.49), calls=%async_computation.5 | async-start | bytes 8388608
  120.5 5.1 slice-start.1
  121.1 4.5 copy-start.12
  166.1 381.2 %all-gather.2.cloned.1.call-start = ((), (), s32[]{:S(2)}) async-start(), calls=%async_computation.3 | async-start | bytes 10485760 | tf_op jit(solution)/shard_map/all_gather | solution.py:77
  388.8 5.0 copy-start.2
  396.5 234.6 %reduce-scatter.5.cloned.1.call-start = ((), (), s32[]{:S(2)}) async-start(), calls=%async_computation.4 | async-start | bytes 7077888 | tf_op jit(solution)/shard_map/reduce_scatter | solution.py:80
  547.3 8.3 %copy-start.13 = (bf16[2048,2048]{0,1:T(8,128)(2,1)S(1)}, bf16[2048,2048]{0,1:T(8,128)(2,1)}, u32[]{:S(2)}) copy-start(bf16[2048,2048]{0,1:T(8,128)(2,1)} %all-gather.2.cloned.1.call-done) | copy-start | bytes 25165828
Sparse Core Ops, SparseCore 0:
  166.2 209.1 reduce-scatter.2
  396.6 150.6 all-gather.1
  571.1 59.9 reduce-scatter.4
